TPU v7x, 8 devices: a whole 2x2x1 slice. The times are simulated.
8 devices in a mesh: dp: 1 (over z), ctx: 8 (over y, x, core).
Axes of the slice: x: 2, y: 2, z: 1, core: 2. Of those that a mesh axis runs over, the one named last changes fastest.
Arguments:
- hidden: bfloat16 [256, 2048], P(('dp', 'ctx'))
- w_q: bfloat16 [2048, 3072], replicated
- w_uk: bfloat16 [16, 128, 512], replicated
- w_uv: bfloat16 [16, 512, 128], replicated
- w_o: bfloat16 [2048, 2048], replicated
- kv_prefix: bfloat16 [16384, 576], P(('dp', 'ctx'))
- kv_suffix: bfloat16 [256, 2048, 576], P(('dp', 'ctx'))
- seq_lens: int32 [256], P(('dp', 'ctx'))
Outputs:
- output: bfloat16 [256, 2048], P(('dp', 'ctx'))
All inputs are finite; a program needn't handle non-finite values.
Results may differ from a plain program's by a relative error of at most 0.00657996.
Values are sent between devices in bfloat16 or wider.
A program may use at most 1 GiB of HBM per device.

v0:
```python
import math
import jax
import jax.numpy as jnp
from jax import lax
from jax.sharding import PartitionSpec as P

ROPE_BASE = 10000


def rope_rotate(rot_in, positions):
    half_dim = rot_in.shape[-1] // 2
    inv_freq = jnp.exp(jnp.arange(half_dim, dtype=jnp.float32) * (-math.log(ROPE_BASE) / half_dim))
    angle = positions.astype(jnp.float32)[:, None, None] * inv_freq
    cos_part = jnp.cos(angle)
    sin_part = jnp.sin(angle)
    rot_wide = rot_in.astype(jnp.float32)
    first_half = rot_wide[..., :half_dim]
    second_half = rot_wide[..., half_dim:]
    return jnp.concatenate([first_half * cos_part - second_half * sin_part, second_half * cos_part + first_half * sin_part], axis=-1)


def make_query(hidden, w_q, w_uk, positions):
    rows = hidden.shape[0]
    heads, nope_dim = w_uk.shape[0], w_uk.shape[1]
    q_all = jnp.dot(hidden, w_q, preferred_element_type=jnp.float32).astype(jnp.bfloat16).reshape(rows, heads, -1)
    q_lat = jnp.einsum('bhn,hnc->bhc', q_all[..., :nope_dim], w_uk, preferred_element_type=jnp.float32).astype(jnp.bfloat16)
    q_rot = rope_rotate(q_all[..., nope_dim:], positions).astype(jnp.bfloat16)
    return jnp.concatenate([q_lat, q_rot], axis=-1)


def suffix_scores(query, kv_suffix, seq_lens, scale):
    s_suf = jnp.einsum('bhw,bsw->bhs', query, kv_suffix, preferred_element_type=jnp.float32) * scale
    slots = jnp.arange(kv_suffix.shape[1])
    return jnp.where(slots[None, None, :] <= seq_lens[:, None, None], s_suf, -jnp.inf)


def finish_output(hidden, o_lat, w_uv, w_o):
    o_val = jnp.einsum('bhc,hcv->bhv', o_lat, w_uv, preferred_element_type=jnp.float32).astype(jnp.bfloat16)
    out_proj = jnp.dot(o_val.reshape(hidden.shape[0], -1), w_o, preferred_element_type=jnp.float32)
    return (hidden.astype(jnp.float32) + out_proj).astype(jnp.bfloat16)


def solution(mesh):
    group = mesh.shape['ctx']
    rows_spec = P(('dp', 'ctx'), None)
    whole_spec = P()

    def local_step(hidden, w_q, w_uk, w_uv, w_o, kv_prefix, kv_suffix, seq_lens):
        rows = hidden.shape[0]
        lat_dim = w_uk.shape[2]
        prefix_len = kv_prefix.shape[0] * group
        scale = (w_q.shape[1] // w_uk.shape[0]) ** -0.5
        query = make_query(hidden, w_q, w_uk, prefix_len + seq_lens)
        q_group = lax.all_gather(query, 'ctx', axis=0, tiled=True)
        s_pre = jnp.einsum('bhw,pw->bhp', q_group, kv_prefix, preferred_element_type=jnp.float32) * scale
        m_pre = lax.pmax(jnp.max(s_pre, axis=-1), 'ctx')
        e_pre = jnp.exp(s_pre - m_pre[..., None])
        l_pre = jnp.sum(e_pre, axis=-1)
        o_pre = jnp.einsum('bhp,pc->bhc', e_pre.astype(jnp.bfloat16), kv_prefix[:, :lat_dim], preferred_element_type=jnp.float32)
        o_home = lax.psum_scatter(o_pre, 'ctx', scatter_dimension=0, tiled=True)
        l_home = lax.psum_scatter(l_pre, 'ctx', scatter_dimension=0, tiled=True)
        m_home = lax.dynamic_slice_in_dim(m_pre, lax.axis_index('ctx') * rows, rows, axis=0)
        s_suf = suffix_scores(query, kv_suffix, seq_lens, scale)
        m_all = jnp.maximum(m_home, jnp.max(s_suf, axis=-1))
        pre_weight = jnp.exp(m_home - m_all)
        e_suf = jnp.exp(s_suf - m_all[..., None])
        norm_sum = l_home * pre_weight + jnp.sum(e_suf, axis=-1)
        suf_part = jnp.einsum('bhs,bsc->bhc', e_suf.astype(jnp.bfloat16), kv_suffix[..., :lat_dim], preferred_element_type=jnp.float32)
        o_lat = ((o_home * pre_weight[..., None] + suf_part) / norm_sum[..., None]).astype(jnp.bfloat16)
        return finish_output(hidden, o_lat, w_uv, w_o)

    return jax.shard_map(local_step, mesh=mesh, in_specs=(rows_spec, whole_spec, whole_spec, whole_spec, whole_spec, rows_spec, P(('dp', 'ctx'), None, None), P(('dp', 'ctx'))), out_specs=rows_spec, check_vma=False)
```

profile of v0, /device:TPU:0, one launch (start us, length us, event | category | flops | bytes accessed | tf_op | source)
XLA Modules:
  0.0 220.7 jit_solution(4245803186042678867)
XLA Ops:
  6.6 7.1 %convolution_convert_fusion = bf16[32,3072]{1,0:T(8,128)(2,1)S(1)} fusion(bf16[32,2048]{1,0:T(8,128)(2,1)} %param.8, bf16[2048,3072]{1,0:T(8,128)(2,1)} %param.9), kind=kOutput, calls=%fused_computation.12 | convolution fusion | flops 402751488 | bytes 12910592 | tf_op jit(solution)/shard_map/dot_general | solution.py:25
  13.6 0.3 reshape.90
  14.1 0.1 multiply_cosine_fusion
  14.2 0.4 fusion.21
  14.6 0.1 subtract_convert_fusion
  14.8 1.0 pad_maximum_fusion
  15.8 0.0 all-gather.2.cloned.1.call-update
  15.8 0.0 reduce-scatter.7.cloned.1.call-start
  15.8 38.1 %all-gather.2.cloned.1.call-done = bf16[256,16,576]{2,0,1:T(8,128)(2,1)} async-done(((bf16[32,16,576]{2,0,1:T(8,128)(2,1)}), bf16[256,16,576]{2,0,1:T(8,128)(2,1)}) %all-gather.2.cloned.1.call-update) | async-done | bytes 4718608 | tf_op jit(solution)/shard_map/all_gather | solution.py:54
  53.9 21.8 %multiply_reduce_fusion = (f32[256,16]{0,1:T(8,128)S(1)}, f32[256,16,2048]{2,0,1:T(8,128)}) fusion(bf16[256,16,576]{2,0,1:T(8,128)(2,1)} %all-gather.2.cloned.1.call-done, bf16[2048,576]{0,1:T(8,128)(2,1)} %param.13), kind=kOutput, calls=%fused_computation.3 | convolution fusion | flops 9680449536 | bytes 40648704 | tf_op jit(solution)/shard_map/bhw,pw->bhp/dot_general | solution.py:55
  75.7 22.3 %pmax.7 = f32[256,16]{0,1:T(8,128)S(1)} all-reduce(f32[256,16]{0,1:T(8,128)S(1)} %get-tuple-element.13), channel_id=1, replica_groups=mesh['dp'=1,'ctx'=8] {'ctx'}, use_global_device_ids=true, to_apply=%region_1.0 | all-reduce | flops 4096 | bytes 32768 | tf_op jit(solution)/shard_map/pmax | solution.py:56
  98.0 14.0 %fusion.2 = f32[256,16]{0,1:T(8,128)S(1)} fusion(f32[256,16,2048]{2,0,1:T(8,128)} %get-tuple-element.14, f32[256,16]{0,1:T(8,128)S(1)} %pmax.7), kind=kLoop, calls=%fused_computation.4 | loop fusion | flops 25161728 | bytes 33587200 | tf_op jit(solution)/shard_map/reduce_sum | solution.py:58
  112.0 0.8 copy.39
  112.7 0.0 reduce-scatter.7.cloned.1.call-update
  112.8 0.2 reduce-scatter.5.cloned.1.call-start
  113.0 17.7 %fusion.4 = f32[256,16,512]{2,0,1:T(8,128)} fusion(f32[256,16,2048]{2,0,1:T(8,128)} %get-tuple-element.14, f32[256,16]{0,1:T(8,128)S(1)} %pmax.7, bf16[2048,576]{0,1:T(8,128)(2,1)} %param.13), kind=kOutput, calls=%fused_computation.6 | convolution fusion | flops 8615100416 | bytes 44056576 | tf_op jit(solution)/shard_map/bhp,pc->bhc/dot_general | solution.py:59
  130.7 0.0 reduce-scatter.5.cloned.1.call-update
  130.7 0.1 iota_compare_fusion
  130.8 0.9 copy-done.2
  131.8 27.7 %fusion.8 = (f32[32,16]{1,0:T(8,128)S(1)}, f32[32,16,2048]{2,1,0:T(8,128)}) fusion(pred[32,2048]{1,0:T(8,128)(4,1)S(1)} %iota_compare_fusion, bf16[32,2048,576]{1,2,0:T(8,128)(2,1)} %param.14, bf16[32,16,576]{2,0,1:T(8,128)(2,1)S(1)} %copy-done.2), kind=kOutput, calls=%fused_computation.11 | convolution fusion | flops 1211104768 | bytes 80349184 | tf_op jit(solution)/shard_map/bhw,bsw->bhs/dot_general | solution.py:32
  159.5 0.1 copy.33
  159.5 0.1 dynamic-slice_maximum_fusion
  159.6 0.1 copy.34
  159.7 3.3 %fusion.9 = f32[32,16]{1,0:T(8,128)S(1)} fusion(f32[32,16,2048]{2,1,0:T(8,128)} %get-tuple-element.12, f32[32,16]{1,0:T(8,128)S(1)} %copy.34, pred[32,2048]{1,0:T(8,128)(4,1)S(1)} %iota_compare_fusion), kind=kLoop, calls=%fused_computation.13 | loop fusion | flops 4193792 | bytes 4263936 | tf_op jit(solution)/shard_map/reduce_sum | solution.py:67
  163.0 0.1 copy.37
  163.0 26.6 %fusion = f32[32,16,512]{2,1,0:T(8,128)S(1)} fusion(bf16[32,2048,576]{1,2,0:T(8,128)(2,1)} %param.14, f32[32,16,2048]{2,1,0:T(8,128)} %get-tuple-element.12, f32[32,16]{1,0:T(8,128)S(1)} %copy.34, pred[32,2048]{1,0:T(8,128)(4,1)S(1)} %iota_compare_fusion), kind=kOutput, calls=%fused_computation | convolution fusion | flops 1077936128 | bytes 72419328 | tf_op jit(solution)/shard_map/bhs,bsc->bhc/dot_general | solution.py:68
  189.6 0.0 reduce-scatter.7.cloned.1.call-done
  189.6 0.8 copy.40
  190.5 0.1 multiply_add_fusion
  190.5 15.1 %reduce-scatter.5.cloned.1.call-done = f32[32,16,512]{2,0,1:T(8,128)} async-done(((f32[256,16,512]{2,0,1:T(8,128)}), f32[32,16,512]{2,0,1:T(8,128)}) %reduce-scatter.5.cloned.1.call-update) | async-done | bytes 1048592 | tf_op jit(solution)/shard_map/reduce_scatter | solution.py:60
  205.7 2.9 %fusion.22 = bf16[16,4,8,128]{3,2,1,0:T(8,128)(2,1)S(1)} fusion(bf16[16,512,128]{2,1,0:T(8,128)(2,1)} %param.11, f32[32,16,512]{2,1,0:T(8,128)S(1)} %fusion, f32[32,16,512]{2,0,1:T(8,128)} %reduce-scatter.5.cloned.1.call-done, f32[32,16]{0,1:T(8,128)S(1)} %get-tuple-element.5, f32[32,16]{0,1:T(8,128)S(1)} %get-tuple-element.6), kind=kOutput, calls=%fused_computation.28 | convolution fusion | flops 68222976 | bytes 4329472 | tf_op jit(solution)/shard_map/bhc,hcv->bhv/dot_general | solution.py:38
  208.6 5.6 %fusion.13 = bf16[32,2048]{1,0:T(8,128)(2,1)} fusion(bf16[2048,2048]{1,0:T(8,128)(2,1)} %param.12, bf16[32,2048]{1,0:T(8,128)(2,1)S(1)} %copy-done.3, bf16[16,4,8,128]{3,2,1,0:T(8,128)(2,1)S(1)} %fusion.22), kind=kOutput, calls=%fused_computation.18 | convolution fusion | flops 268632064 | bytes 8781824 | tf_op jit(solution)/shard_map/dot_general | solution.py:39
  (15 shorter events, 0.1 us)
Async XLA Ops:
  6.5 7.7 %copy-start = (bf16[16,128,512]{2,1,0:T(8,128)(2,1)S(1)}, bf16[16,128,512]{2,1,0:T(8,128)(2,1)}, u32[]{:S(2)}) copy-start(bf16[16,128,512]{2,1,0:T(8,128)(2,1)} %param.10) | copy-start | bytes 6291460
  6.5 47.4 %all-gather.2.cloned.1.call-start = ((), (), s32[]{:S(2)}) async-start(), calls=%async_computation.2 | async-start | bytes 5898240 | tf_op jit(solution)/shard_map/all_gather | solution.py:54
  6.5 7.5 %copy-start.4 = (s32[32]{0:T(128)S(1)}, s32[32]{0:T(128)}, u32[]{:S(2)}) copy-start(s32[32]{0:T(128)} %param.15) | copy-start | bytes 388
  15.8 173.9 %reduce-scatter.7.cloned.1.call-start = ((), (), s32[]{:S(2)}) async-start(), calls=%async_computation.4 | async-start | bytes 147456
  112.8 92.9 %reduce-scatter.5.cloned.1.call-start = ((), (), s32[]{:S(2)}) async-start(), calls=%async_computation.3 | async-start | bytes 9437184 | tf_op jit(solution)/shard_map/reduce_scatter | solution.py:60
  130.7 1.1 copy-start.2
  189.6 18.9 %copy-start.3 = (bf16[32,2048]{1,0:T(8,128)(2,1)S(1)}, bf16[32,2048]{1,0:T(8,128)(2,1)}, u32[]{:S(2)}) copy-start(bf16[32,2048]{1,0:T(8,128)(2,1)} %param.8) | copy-start | bytes 393220
  205.7 8.5 %copy-start.1 = (bf16[16,128,512]{2,1,0:T(8,128)(2,1)S(1)}, bf16[16,128,512]{2,1,0:T(8,128)(2,1)}, u32[]{:S(2)}) copy-start(bf16[16,128,512]{2,1,0:T(8,128)(2,1)} %param.10) | copy-start | bytes 6291460
Sparse Core Ops, SparseCore 0:
  15.9 37.9 all-gather.1
  112.9 26.9 reduce-scatter.6
  143.3 62.3 reduce-scatter.4
where the time goes:
time: 221 us
  matrix products  110 us (50%)
  waiting for transfers between devices  53.3 us (24%)
  blocking collectives  22.3 us (10%)
  other arithmetic  18.9 us (9%)
  between operations  13.3 us (6%)
  local copies, waits for them, and re-layouts  3.11 us (1%)
    all_gather x1, waiting for transfers between devices, local_step(): q_group = lax.all_gather(query, 'ctx', axis=0, tiled=True)  38.1 us
    dot_general x1, matrix products, suffix_scores(): jnp.einsum('bhw,bsw->bhs', query, kv_suffix, preferred_element_type=jnp.f...  27.7 us
    dot_general x1, matrix products, local_step(): jnp.einsum('bhs,bsc->bhc', e_suf.astype(jnp.bfloat16), kv_suffix[..., :la...  26.6 us
    pmax x1, blocking collectives, local_step(): m_pre = lax.pmax(jnp.max(s_pre, axis=-1), 'ctx')  22.3 us
    dot_general x1, matrix products, local_step(): jnp.einsum('bhw,pw->bhp', q_group, kv_prefix, preferred_element_type=jnp....  21.8 us
    dot_general x1, matrix products, local_step(): jnp.einsum('bhp,pc->bhc', e_pre.astype(jnp.bfloat16), kv_prefix[:, :lat_d...  17.7 us
    reduce_scatter x1, waiting for transfers between devices, local_step(): o_home = lax.psum_scatter(o_pre, 'ctx', scatter_dimension=0, tiled=True)  15.1 us
    reduce_sum x1, other arithmetic, local_step(): l_pre = jnp.sum(e_pre, axis=-1)  14 us
  transfers between devices with their start and end apart: 3, of which 2 were waited for; matrix products, arithmetic and copies ran while one was open for 35% of the time, Pallas kernels for 0%

commit v1 on v0

v1 whole, which is shorter than its diff:
```python
import functools
import math
import jax
import jax.numpy as jnp
from jax import lax
from jax.experimental import pallas as pl
from jax.experimental.pallas import tpu as pltpu
from jax.sharding import PartitionSpec as P

ROPE_BASE = 10000
LOG2E = 1.4426950408889634
NT = (((1,), (1,)), ((), ()))
F32 = jnp.float32
BF16 = jnp.bfloat16
MIB = 1024 * 1024
TAIL = 8


def vmem():
    return pl.BlockSpec(memory_space=pltpu.VMEM)


def hbm():
    return pl.BlockSpec(memory_space=pl.ANY)


def wide(x, n):
    return jnp.concatenate([x] * n, axis=1)


def prefix_kernel(n_head, nope, rope, log2_scale, hid_ref, cos_ref, sin_ref, wq_hbm, wuk_hbm, kv_hbm,
                  qs_ref, own_ref, x_ref, y_ref,
                  hid_all, cos_all, sin_all, wq_v, wuk_v, kv_v, q_v, qs_f, m_v, l_v, s_v, p_v, diag, carry,
                  wq_sem, own_sem, send_sem, recv_sem):
    rows = hid_ref.shape[0]
    lat = wuk_v.shape[2]
    qk = nope + rope
    per = 4
    groups = n_head // per
    width = per * qk
    half = n_head // 2
    block = half * rows
    chunk = s_v.shape[2]
    me = lax.axis_index('ctx')
    core = lax.rem(me, 2)
    xx = lax.rem(me // 2, 2)
    yy = me // 4
    sib = me + 1 - 2 * core
    to_x = me + 2 - 4 * xx
    to_y = me + 4 - 8 * yy
    to_d = me + 6 - 4 * xx - 8 * yy
    weights = []
    for g in range(groups):
        cols = pl.ds(g * width, width)
        weights.append(pltpu.make_async_copy(wq_hbm.at[:, cols], wq_v.at[:, cols], wq_sem.at[g]))
    wuk_copy = pltpu.make_async_copy(wuk_hbm, wuk_v, own_sem.at[0])
    kv_copy = pltpu.make_async_copy(kv_hbm, kv_v.at[0], own_sem.at[1])
    for copy in (weights[0], wuk_copy, *weights[1:], kv_copy):
        copy.start()

    barrier = pltpu.get_barrier_semaphore()
    for peer in (sib, to_x, to_y, to_d):
        pl.semaphore_signal(barrier, inc=1, device_id={'ctx': peer})
    pl.semaphore_wait(barrier, 4)

    def remote(src, dst, n, peer):
        return pltpu.make_async_remote_copy(
            src_ref=src, dst_ref=dst, send_sem=send_sem.at[n], recv_sem=recv_sem.at[n], device_id={'ctx': peer})

    gathers = []
    for slot, peer in ((2, to_d), (0, to_x), (1, to_y)):
        gathers.append(remote(hid_ref, hid_all.at[slot], slot, peer))
        gathers.append(remote(cos_ref, cos_all.at[slot], 3 + slot, peer))
        gathers.append(remote(sin_ref, sin_all.at[slot], 6 + slot, peer))
    kv_send = remote(kv_hbm, kv_v.at[1], 9, sib)
    for copy in (*gathers, kv_send):
        copy.start()

    i = lax.broadcasted_iota(jnp.int32, (rope, rope), 0)
    j = lax.broadcasted_iota(jnp.int32, (rope, rope), 1)
    rot = jnp.where(i == j + rope // 2, -1.0, jnp.where(i + rope // 2 == j, 1.0, 0.0)).astype(BF16)

    def project(hid, cos, sin, g, store):
        q_all = jnp.dot(hid, wq_v[:, g * width:(g + 1) * width], preferred_element_type=F32)
        for n in range(per):
            q_nope = q_all[:, n * qk:n * qk + nope].astype(BF16)
            q_pe = q_all[:, n * qk + nope:(n + 1) * qk].astype(BF16)
            q_lat = jnp.dot(q_nope, wuk_v[g * per + n], preferred_element_type=F32).astype(BF16)
            turned = jnp.dot(q_pe, rot, preferred_element_type=F32)
            q_rot = (q_pe.astype(F32) * wide(cos, 2) + turned * wide(sin, 2)).astype(BF16)
            store(g * per + n, q_lat, q_rot)

    def keep(peer, h, q_lat, q_rot):
        at = slice((h % half) * rows, (h % half + 1) * rows)
        q_v[2 * peer + h // half, at, 0:lat] = q_lat
        q_v[2 * peer + h // half, at, lat:lat + rope] = q_rot

    def store_own(h, q_lat, q_rot):
        keep(3, h, q_lat, q_rot)
        for n in range(lat // 128):
            qs_f[n, pl.ds(h, rows, stride=n_head), :] = q_lat[:, n * 128:(n + 1) * 128].astype(F32)
        qs_f[lat // 128, pl.ds(h, rows, stride=n_head), :] = wide(q_rot, 2).astype(F32)

    def store_peer(h, q_lat, q_rot):
        for p in range(3):
            keep(p, h, q_lat[p * rows:(p + 1) * rows], q_rot[p * rows:(p + 1) * rows])

    def attend(peer, o_ref):
        for n in range(2):
            o_ref[n, 0:block] = jnp.zeros((block, lat), F32)
            m_v[2 * peer + n] = jnp.full((block, 128), -jnp.inf, F32)
            l_v[2 * peer + n] = jnp.zeros((block, 128), F32)

        def visit(i, _):
            keys = pl.ds(pl.multiple_of(i * chunk, chunk), chunk)
            items = [(k, n) for k in range(2) for n in range(2)]
            for t, (k, n) in enumerate(items):
                s_v[t] = jnp.dot(q_v[2 * peer + n], kv_v[k, :, keys], preferred_element_type=F32)
            for t, (k, n) in enumerate(items):
                b = 2 * peer + n
                for r in range(0, block, 64):
                    at = slice(r, r + 64)
                    s = s_v[t, at]
                    m_old = m_v[b, at]
                    m_new = jnp.maximum(m_old, jnp.max(s, axis=1, keepdims=True))
                    alpha = jnp.exp2((m_old - m_new) * log2_scale)
                    p = jnp.exp2((s - wide(m_new, chunk // 128)) * log2_scale)
                    part = p[:, 0:128]
                    for c in range(1, chunk // 128):
                        part += p[:, c * 128:(c + 1) * 128]
                    l_v[b, at] = l_v[b, at] * alpha + part
                    m_v[b, at] = m_new
                    p_v[t, at] = p.astype(BF16)
                    o_ref[n, at] = o_ref[n, at] * wide(alpha, lat // 128)
                o_ref[n, 0:block] += lax.dot_general(p_v[t], kv_v[k, 0:lat, keys], NT, preferred_element_type=F32)
            return 0

        lax.fori_loop(0, kv_v.shape[2] // chunk, visit, 0)

    def close(peer, o_ref):
        for n in range(2):
            b = 2 * peer + n
            o_ref[n, block:block + TAIL, 0:block] = jnp.transpose(m_v[b])[0:TAIL]
            l_sum = jnp.broadcast_to(jnp.sum(l_v[b], axis=1, keepdims=True), (block, 128))
            o_ref[n, block:block + TAIL, block:2 * block] = jnp.transpose(l_sum)[0:TAIL]

    def merge(peer, n, o_ref, c):
        b = 2 * peer + n
        m_in = jnp.broadcast_to(jnp.transpose(carry[c, block:block + TAIL, 0:block])[:, 0:1], (block, 128))
        l_in = jnp.transpose(carry[c, block:block + TAIL, block:2 * block])[:, 0:1]
        m_new = jnp.maximum(m_v[b], m_in)
        mine = jnp.exp2((m_v[b] - m_new) * log2_scale)
        theirs = jnp.exp2((m_in - m_new) * log2_scale)
        first_lane = lax.broadcasted_iota(jnp.int32, (block, 128), 1) == 0
        l_v[b] = l_v[b] * mine + jnp.where(first_lane, l_in * theirs, 0.0)
        m_v[b] = m_new
        o_ref[n, 0:block] = o_ref[n, 0:block] * wide(mine, lat // 128) + carry[c, 0:block] * wide(theirs, lat // 128)

    for g in range(groups):
        weights[g].wait()
        if g == 0:
            wuk_copy.wait()
        project(hid_ref[...], cos_ref[...], sin_ref[...], g, store_own)
    for n in range(lat // 128):
        qs_ref[:, n * 128:(n + 1) * 128] = qs_f[n].astype(BF16)
    qs_ref[:, lat:lat + rope] = qs_f[lat // 128][:, 0:rope].astype(BF16)
    kv_copy.wait()
    kv_send.wait()
    attend(3, own_ref)
    close(3, own_ref)

    for copy in gathers:
        copy.wait()
    hid3 = hid_all[...].reshape(3 * rows, hid_ref.shape[1])
    cos3 = jnp.concatenate([cos_all[p] for p in range(3)], axis=0)
    sin3 = jnp.concatenate([sin_all[p] for p in range(3)], axis=0)
    for g in range(groups):
        project(hid3, cos3, sin3, g, store_peer)

    attend(2, diag)
    close(2, diag)
    over = [remote(diag.at[0], carry.at[0], 10, to_x), remote(diag.at[1], carry.at[1], 11, to_y)]
    for copy in over:
        copy.start()
    attend(0, x_ref)
    attend(1, y_ref)
    for copy in over:
        copy.wait()
    merge(1, 0, y_ref, 0)
    merge(0, 1, x_ref, 1)
    close(0, x_ref)
    close(1, y_ref)


def prefix_phase(hidden, w_q, w_uk, kv_own, seq_lens, first_pos, log2_scale, chunk=1024):
    rows, dim = hidden.shape
    n_head, nope, lat = w_uk.shape
    qk = w_q.shape[1] // n_head
    rope = qk - nope
    inv_freq = jnp.exp(jnp.arange(rope // 2, dtype=F32) * (-math.log(ROPE_BASE) / (rope // 2)))
    angle = (first_pos + seq_lens).astype(F32)[:, None] * inv_freq
    block = n_head // 2 * rows
    payload = jax.ShapeDtypeStruct((2, block + TAIL, lat), F32)
    in_hbm = pl.BlockSpec(memory_space=pltpu.HBM)
    return pl.pallas_call(
        functools.partial(prefix_kernel, n_head, nope, rope, log2_scale),
        out_shape=(jax.ShapeDtypeStruct((rows * n_head, lat + rope), BF16), payload, payload, payload),
        in_specs=[vmem(), vmem(), vmem(), in_hbm, in_hbm, in_hbm],
        out_specs=(vmem(), vmem(), vmem(), vmem()),
        scratch_shapes=[
            pltpu.VMEM((3, rows, dim), BF16), pltpu.VMEM((3, rows, rope // 2), F32), pltpu.VMEM((3, rows, rope // 2), F32),
            pltpu.VMEM(w_q.shape, BF16), pltpu.VMEM(w_uk.shape, BF16), pltpu.VMEM((2, *kv_own.shape), BF16),
            pltpu.VMEM((8, block, lat + rope), BF16), pltpu.VMEM((lat // 128 + 1, rows * n_head, 128), F32),
            pltpu.VMEM((8, block, 128), F32), pltpu.VMEM((8, block, 128), F32),
            pltpu.VMEM((4, block, chunk), F32), pltpu.VMEM((4, block, chunk), BF16),
            pltpu.VMEM(payload.shape, F32), pltpu.VMEM(payload.shape, F32),
            pltpu.SemaphoreType.DMA((n_head // 4,)), pltpu.SemaphoreType.DMA((2,)),
            pltpu.SemaphoreType.DMA((12,)), pltpu.SemaphoreType.DMA((12,))],
        compiler_params=pltpu.CompilerParams(collective_id=0, has_side_effects=True, vmem_limit_bytes=60 * MIB),
        name='prefix',
    )(hidden, jnp.cos(angle), jnp.sin(angle), w_q, w_uk, kv_own)


def suffix_kernel(log2_scale, lat, chunk, unit, ring, lens_ref, q_ref, kv_hbm, o_ref, m_ref, l_ref,
                  kv_v, s_v, m_v, l_v, acc, sems, b_s, c_s):
    n_seq = lens_ref.shape[0]
    heads = q_ref.shape[0] // n_seq
    shift = chunk.bit_length() - 1
    total = jnp.int32(0)
    for b in range(n_seq):
        total += lax.shift_right_logical(lens_ref[b], shift) + 1
    trips = lax.div(total + unit - 1, unit)
    depth = ring - 2

    def start(at, group):
        b, c = at
        for u in range(unit):
            b_s[group * unit + u] = b
            c_s[group * unit + u] = c
            have = jnp.minimum(b, n_seq - 1)
            pltpu.make_async_copy(
                kv_hbm.at[have, :, pl.ds(pl.multiple_of(c * chunk, chunk), chunk)], kv_v.at[group, u], sems.at[group]).start()
            last = c >= lax.shift_right_logical(lens_ref[have], shift)
            b, c = jnp.where(last, jnp.minimum(b + 1, n_seq), b), jnp.where(last, 0, c + 1)
        return b, c

    for u in range(unit):
        b_s[(ring - 1) * unit + u] = n_seq
        c_s[(ring - 1) * unit + u] = 0
    ahead = lax.fori_loop(0, jnp.minimum(depth, trips), lambda j, at: start(at, j), (jnp.int32(0), jnp.int32(0)))

    def step(i, at):
        base, prev, far = [lax.rem(i + d, ring) for d in (0, ring - 1, depth)]
        at = lax.cond(i + depth < trips, lambda: start(at, far), lambda: at)

        @pl.when(i < trips)
        def _():
            pltpu.make_async_copy(kv_v.at[base], kv_v.at[base], sems.at[base]).wait()

        here, there = lax.rem(i, 2), lax.rem(i + 1, 2)
        for u in range(unit):
            bq = jnp.minimum(b_s[base * unit + u], n_seq - 1)
            q = q_ref[pl.ds(pl.multiple_of(bq * heads, heads), heads), :]
            s_v[here, u] = jnp.dot(q, kv_v[base, u], preferred_element_type=F32)

        lanes = lax.broadcasted_iota(jnp.int32, (heads, chunk), 1)
        items = [(b_s[prev * unit + u], c_s[prev * unit + u]) for u in range(unit)]
        scores = []
        for u, (b, c) in enumerate(items):
            length = lens_ref[jnp.minimum(b, n_seq - 1)]
            scores.append(jnp.where(lanes <= length - c * chunk, s_v[there, u], -jnp.inf))
        top = jnp.max(jnp.concatenate(scores, axis=0), axis=1, keepdims=True)
        m_old, l_old, o_old = m_v[...], l_v[...], acc[...]
        for u, (b, c) in enumerate(items):
            first = c == 0
            m_old = jnp.where(first, -jnp.inf, m_old)
            m_new = jnp.maximum(m_old, top[u * heads:(u + 1) * heads])
            alpha = jnp.exp2((m_old - m_new) * log2_scale)
            p = jnp.exp2((scores[u] - wide(m_new, chunk // 128)) * log2_scale)
            part = p[:, 0:128]
            for n in range(1, chunk // 128):
                part += p[:, n * 128:(n + 1) * 128]
            added = lax.dot_general(p.astype(BF16), kv_v[prev, u, 0:lat, :], NT, preferred_element_type=F32)
            l_old = jnp.where(first, 0.0, l_old * alpha) + part
            o_old = jnp.where(first, 0.0, o_old * wide(alpha, lat // 128)) + added
            m_old = m_new
            out = pl.ds(pl.multiple_of(b * heads, heads), heads)
            m_ref[out, :] = m_old
            l_ref[out, :] = l_old
            for n in range(lat // 128):
                o_ref[n, out, :] = o_old[:, n * 128:(n + 1) * 128]
        m_v[...], l_v[...], acc[...] = m_old, l_old, o_old
        return at

    lax.fori_loop(0, trips + 1, step, ahead)


def suffix_part(q_seq, kv_suffix, seq_lens, log2_scale, lat, chunk=256, unit=8, ring=5):
    n_seq, slots, wide_row = kv_suffix.shape
    rows = q_seq.shape[0]
    heads = rows // n_seq
    flops = 2 * rows * slots * (wide_row + lat) * 4
    return pl.pallas_call(
        functools.partial(suffix_kernel, log2_scale, lat, chunk, unit, ring),
        out_shape=(jax.ShapeDtypeStruct((lat // 128, rows + heads, 128), F32), jax.ShapeDtypeStruct((rows + heads, 128), F32),
                   jax.ShapeDtypeStruct((rows + heads, 128), F32)),
        in_specs=[pl.BlockSpec(memory_space=pltpu.SMEM), vmem(), hbm()],
        out_specs=(vmem(), vmem(), vmem()),
        scratch_shapes=[pltpu.VMEM((ring, unit, wide_row, chunk), BF16), pltpu.VMEM((2, unit, heads, chunk), F32),
                        pltpu.VMEM((heads, 128), F32), pltpu.VMEM((heads, 128), F32),
                        pltpu.VMEM((heads, lat), F32), pltpu.SemaphoreType.DMA((ring,)),
                        pltpu.SMEM((ring * unit,), jnp.int32), pltpu.SMEM((ring * unit,), jnp.int32)],
        compiler_params=pltpu.CompilerParams(vmem_limit_bytes=32 * MIB),
        cost_estimate=pl.CostEstimate(flops=flops, bytes_accessed=40 * MIB, transcendentals=0),
        name='suffix',
    )(seq_lens, q_seq, kv_suffix.swapaxes(1, 2))


def output_kernel(log2_scale, hid_ref, wuv_ref, wo_ref, so_ref, sm_ref, sl_ref, own_ref, x_ref, y_ref, out_ref, v_v):
    n_head = wuv_ref.shape[0]
    rows = hid_ref.shape[0]
    half = n_head // 2
    block = half * rows
    value = wuv_ref.shape[2]
    parts = [[(own_ref, n), (x_ref, n), (y_ref, n)] for n in range(2)]
    cols = []
    for side in parts:
        for ref, n in side:
            m_t = jnp.transpose(ref[n, block:block + TAIL, 0:block])
            l_t = jnp.transpose(ref[n, block:block + TAIL, block:2 * block])
            cols.append((m_t[:, 0:1], l_t[:, 0:1]))
    for h in range(n_head):
        side, at = h // half, (h % half) * rows
        mine = pl.ds(h, rows, stride=n_head)
        own = jnp.concatenate([so_ref[n, mine, :] for n in range(so_ref.shape[0])], axis=1)
        terms = [(own, sm_ref[mine, :][:, 0:1], jnp.sum(sl_ref[mine, :], axis=1, keepdims=True))]
        for k, (ref, n) in enumerate(parts[side]):
            m_part, l_part = cols[side * 3 + k]
            terms.append((ref[n, at:at + rows, :], m_part[at:at + rows], l_part[at:at + rows]))
        m_all = functools.reduce(jnp.maximum, [t[1] for t in terms])
        o_sum, l_sum = 0.0, 0.0
        for o_part, m_part, l_part in terms:
            weight = jnp.exp2((m_part - m_all) * log2_scale)
            o_sum += o_part * weight
            l_sum += l_part * weight
        o_lat = (o_sum / l_sum).astype(BF16)
        v_v[:, h * value:(h + 1) * value] = jnp.dot(o_lat, wuv_ref[h], preferred_element_type=F32).astype(BF16)
    out = hid_ref[...].astype(F32) + jnp.dot(v_v[...], wo_ref[...], preferred_element_type=F32)
    out_ref[...] = out.astype(BF16)


def finish_output(hidden, w_uv, w_o, suffix, parts, log2_scale):
    return pl.pallas_call(
        functools.partial(output_kernel, log2_scale),
        out_shape=jax.ShapeDtypeStruct(hidden.shape, BF16),
        in_specs=[vmem()] * 9,
        out_specs=vmem(),
        scratch_shapes=[pltpu.VMEM((hidden.shape[0], w_o.shape[0]), BF16)],
        compiler_params=pltpu.CompilerParams(vmem_limit_bytes=32 * MIB),
        name='output',
    )(hidden, w_uv, w_o, *suffix, *parts)


def solution(mesh):
    group = mesh.shape['ctx']
    rows_spec = P(('dp', 'ctx'), None)
    whole_spec = P()
    over_x = [(i, i ^ 2) for i in range(group)]
    over_y = [(i, i ^ 4) for i in range(group)]

    def local_step(hidden, w_q, w_uk, w_uv, w_o, kv_prefix, kv_suffix, seq_lens):
        lat = w_uk.shape[2]
        n_head = w_uk.shape[0]
        log2_scale = LOG2E * (w_q.shape[1] // n_head) ** -0.5
        kv_own = kv_prefix.swapaxes(0, 1)
        q_seq, own, to_x, to_y = prefix_phase(hidden, w_q, w_uk, kv_own, seq_lens, kv_prefix.shape[0] * group, log2_scale)
        got_x, got_y = lax.ppermute(to_x, 'ctx', over_x), lax.ppermute(to_y, 'ctx', over_y)
        suffix = suffix_part(q_seq, kv_suffix, seq_lens, log2_scale, lat)
        return finish_output(hidden, w_uv, w_o, suffix, (own, got_x, got_y), log2_scale)

    return jax.shard_map(local_step, mesh=mesh, in_specs=(rows_spec, whole_spec, whole_spec, whole_spec, whole_spec, rows_spec, P(('dp', 'ctx'), None, None), P(('dp', 'ctx'))), out_specs=rows_spec, check_vma=False)
```

time: 221 us -> 75.2 us (0.34)
  matrix products: 110 us -> 0 us
  Pallas kernels: 0 us -> 66.3 us
  waiting for transfers between devices: 53.3 us -> 4.04 us
  blocking collectives: 22.3 us -> 0 us
  other arithmetic: 18.9 us -> 1.42 us
  between operations: 13.3 us -> 0.06 us
    dot_general x8 -> x0, matrix products: 110 us -> none  [the longest x1 27.7 us: suffix_scores(): jnp.einsum('bhw,bsw->bhs', query, kv_suffix, preferred_element_type=jnp.f...]
    pallas_call x0 -> x3, Pallas kernels: none -> 66.3 us  [the longest x1 43.6 us: prefix_phase(): pl.pallas_call(functools.partial(prefix_kernel, n_head, nope, rope, log2_...]
    all_gather x1 -> x0, waiting for transfers between devices: 38.1 us -> none  [local_step(): q_group = lax.all_gather(query, 'ctx', axis=0, tiled=True)]
    pmax x1 -> x0, blocking collectives: 22.3 us -> none  [local_step(): m_pre = lax.pmax(jnp.max(s_pre, axis=-1), 'ctx')]
    reduce_sum x2 -> x0, other arithmetic: 17.3 us -> none  [the longest x1 14 us: local_step(): l_pre = jnp.sum(e_pre, axis=-1)]
    reduce_scatter x1 -> x0, waiting for transfers between devices: 15.1 us -> none  [local_step(): o_home = lax.psum_scatter(o_pre, 'ctx', scatter_dimension=0, tiled=True)]
    ppermute x0 -> x2, waiting for transfers between devices: none -> 4.04 us  [the longest x1 2.83 us: local_step(): lax.ppermute(to_x, 'ctx', over_x)]
  transfers between devices with their start and end apart: 3 -> 2, of which waited for: 2 -> 2; matrix products, arithmetic and copies ran while one was open for 35% -> 0% of each run, Pallas kernels for 0% -> 25%
where the time goes in v1:
time: 75.2 us; the launch traced here: 75.1 us
  Pallas kernels  66.3 us (88%)
  waiting for transfers between devices  4.04 us (5%)
  starting transfers between devices  2.05 us (3%)
  other arithmetic  1.42 us (2%)
  local copies, waits for them, and re-layouts  1.26 us (2%)
    pallas_call x1, Pallas kernels, prefix_phase(): pl.pallas_call(functools.partial(prefix_kernel, n_head, nope, rope, log2_...  43.6 us
    pallas_call x1, Pallas kernels, suffix_part(): pl.pallas_call(functools.partial(suffix_kernel, log2_scale, lat, chunk, u...  18.9 us
    pallas_call x1, Pallas kernels, finish_output(): pl.pallas_call(functools.partial(output_kernel, log2_scale), out_shape=ja...  3.78 us
    ppermute x1, waiting for transfers between devices, local_step(): lax.ppermute(to_x, 'ctx', over_x)  2.83 us
    ppermute x1, starting transfers between devices, local_step(): lax.ppermute(to_x, 'ctx', over_x)  1.51 us
  transfers between devices with their start and end apart: 2, of which 2 were waited for; matrix products, arithmetic and copies ran while one was open for 0% of the time, Pallas kernels for 25%

profile of v1, /device:TPU:0, one launch (start us, length us, event | category | flops | bytes accessed | tf_op | source)
XLA Modules:
  0.0 75.1 jit_solution(6170067004193658198)
XLA Ops:
  0.0 0.7 add_convert_fusion
  0.7 0.8 %multiply_sine_fusion = (f32[32,32]{1,0:T(8,128)}, f32[32,32]{1,0:T(8,128)}) fusion(f32[32]{0:T(128)S(1)} %multiply_exponential_fusion, f32[32]{0:T(128)S(1)} %add_convert_fusion), kind=kLoop, calls=%fused_computation | loop fusion | flops 1024 | bytes 8448 | tf_op jit(solution)/shard_map/sin | solution.py:221
  1.4 0.0 copy-start.4
  1.4 43.6 %prefix.1 = (bf16[512,576]{1,0:T(8,128)(2,1)}, f32[2,264,512]{2,1,0:T(8,128)}, f32[2,264,512]{2,1,0:T(8,128)}, f32[2,264,512]{2,1,0:T(8,128)}) custom-call(bf16[32,2048]{1,0:T(8,128)(2,1)} %hid_ref.3, f32[32,32]{1,0:T(8,128)} %get-tuple-element.20.cos_ref, f32[32,32]{1,0:T(8,128)} %get-tuple-element.19.sin_ref, bf16[2048,3072]{1,0:T(8,128)(2,1)} %wq_hbm.1, ...), custom_call_target="tpu_custom_call" | custom-call | tf_op jit(solution)/shard_map/prefix/pallas_call | solution.py:205
  45.0 1.5 %collective-permute-start = (f32[2,264,512]{2,1,0:T(8,128)}, f32[2,264,512]{2,1,0:T(8,128)S(1)}, u32[]{:S(2)}, u32[]{:S(2)}) collective-permute-start(f32[2,264,512]{2,1,0:T(8,128)} %get-tuple-element.17), channel_id=1, source_target_pairs={{0,2},{1,3},{2,0},{3,1},{4,6},{5,7},{6,4},{7,5}} | collective-permute-start | bytes 3244040 | tf_op jit(solution)/shard_map/ppermute | solution.py:377
  46.5 0.5 collective-permute-start.1
  47.1 0.0 slice-start
  47.1 0.0 copy-done.4
  47.1 0.0 copy-start.2
  47.1 1.2 %copy-done.2 = bf16[512,576]{1,0:T(8,128)(2,1)S(1)} copy-done((bf16[512,576]{1,0:T(8,128)(2,1)S(1)}, bf16[512,576]{1,0:T(8,128)(2,1)}, u32[]{:S(2)}) %copy-start.2) | copy-done | bytes 589848
  48.3 0.0 slice-start.1
  48.3 0.0 copy-start
  48.3 0.0 copy-start.1
  48.3 0.0 copy-start.3
  48.3 18.9 %suffix.1 = (f32[4,528,128]{2,1,0:T(8,128)S(1)}, f32[528,128]{1,0:T(8,128)S(1)}, f32[528,128]{1,0:T(8,128)S(1)}) custom-call(s32[32]{0:T(128)S(1)} %copy-done.4, bf16[512,576]{1,0:T(8,128)(2,1)S(1)} %copy-done.2, bf16[32,576,2048]{2,1,0:T(8,128)(2,1)} %bitcast.1.kv_hbm), custom_call_target="tpu_custom_call" | custom-call | flops 9126805504 | bytes 41943040 | tf_op jit(solution)/shard_map/suffix/pallas_call | solution.py:303
  67.2 2.8 %collective-permute-done.x_ref = f32[2,264,512]{2,1,0:T(8,128)S(1)} collective-permute-done((f32[2,264,512]{2,1,0:T(8,128)}, f32[2,264,512]{2,1,0:T(8,128)S(1)}, u32[]{:S(2)}, u32[]{:S(2)}) %collective-permute-start) | collective-permute-done | bytes 1081376 | tf_op jit(solution)/shard_map/ppermute | solution.py:377
  70.1 1.2 %collective-permute-done.1.y_ref = f32[2,264,512]{2,1,0:T(8,128)S(1)} collective-permute-done((f32[2,264,512]{2,1,0:T(8,128)}, f32[2,264,512]{2,1,0:T(8,128)S(1)}, u32[]{:S(2)}, u32[]{:S(2)}) %collective-permute-start.1) | collective-permute-done | bytes 1081376 | tf_op jit(solution)/shard_map/ppermute | solution.py:377
  71.3 0.0 slice-done
  71.3 0.0 slice-done.1
  71.3 0.0 copy-done
  71.3 0.0 copy-done.1
  71.3 0.0 copy-done.3
  71.3 3.8 %output.1 = bf16[32,2048]{1,0:T(8,128)(2,1)} custom-call(bf16[32,2048]{1,0:T(8,128)(2,1)S(1)} %copy-done.3, bf16[16,512,128]{2,1,0:T(8,128)(2,1)S(1)} %copy-done, bf16[2048,2048]{1,0:T(8,128)(2,1)S(1)} %bitcast.3, f32[4,528,128]{2,1,0:T(8,128)S(1)} %get-tuple-element.13.so_ref, f32[528,128]{1,0:T(8,128)S(1)} %get-tuple-element.14.sm_ref, ...), custom_call_target="tpu_custom_call" | custom-call | tf_op jit(solution)/shard_map/output/pallas_call | solution.py:353
  (2 shorter events, 0.0 us)
Async XLA Ops:
  1.4 45.6 %copy-start.4 = (s32[32]{0:T(128)S(1)}, s32[32]{0:T(128)}, u32[]{:S(2)}) copy-start(s32[32]{0:T(128)} %lens_ref.1) | copy-start | bytes 388
  45.0 25.0 %collective-permute-start = (f32[2,264,512]{2,1,0:T(8,128)}, f32[2,264,512]{2,1,0:T(8,128)S(1)}, u32[]{:S(2)}, u32[]{:S(2)}) collective-permute-start(f32[2,264,512]{2,1,0:T(8,128)} %get-tuple-element.17), channel_id=1, source_target_pairs={{0,2},{1,3},{2,0},{3,1},{4,6},{5,7},{6,4},{7,5}} | collective-permute-start | bytes 3244040 | tf_op jit(solution)/shard_map/ppermute | solution.py:377
  46.5 24.7 %collective-permute-start.1 = (f32[2,264,512]{2,1,0:T(8,128)}, f32[2,264,512]{2,1,0:T(8,128)S(1)}, u32[]{:S(2)}, u32[]{:S(2)}) collective-permute-start(f32[2,264,512]{2,1,0:T(8,128)} %get-tuple-element.18), channel_id=1, source_target_pairs={{0,4},{1,5},{2,6},{3,7},{4,0},{5,1},{6,2},{7,3}} | collective-permute-start | bytes 3244040 | tf_op jit(solution)/shard_map/ppermute | solution.py:377
  47.1 24.2 %slice-start = ((s8[8388608]{0:T(1024)(128)(4,1)}), s8[4194304]{0:T(1024)(128)(4,1)S(1)}, s32[]{:S(2)}) async-start(s8[8388608]{0:T(1024)(128)(4,1)} %bitcast.2), calls=%async_computation | async-start | bytes 8388608
  47.1 1.2 %copy-start.2 = (bf16[512,576]{1,0:T(8,128)(2,1)S(1)}, bf16[512,576]{1,0:T(8,128)(2,1)}, u32[]{:S(2)}) copy-start(bf16[512,576]{1,0:T(8,128)(2,1)} %get-tuple-element.12.q_ref) | copy-start | bytes 1769476
  48.3 23.0 %slice-start.1 = ((s8[8388608]{0:T(1024)(128)(4,1)}), s8[4194304]{0:T(1024)(128)(4,1)S(1)}, s32[]{:S(2)}) async-start(s8[8388608]{0:T(1024)(128)(4,1)} %bitcast.2), calls=%async_computation.1 | async-start | bytes 8388608
  48.3 23.0 %copy-start = (bf16[16,512,128]{2,1,0:T(8,128)(2,1)S(1)}, bf16[16,512,128]{2,1,0:T(8,128)(2,1)}, u32[]{:S(2)}) copy-start(bf16[16,512,128]{2,1,0:T(8,128)(2,1)} %wuv_ref.1) | copy-start | bytes 6291460
  48.3 23.0 %copy-start.1 = (f32[2,264,512]{2,1,0:T(8,128)S(1)}, f32[2,264,512]{2,1,0:T(8,128)}, u32[]{:S(2)}) copy-start(f32[2,264,512]{2,1,0:T(8,128)} %get-tuple-element.16.own_ref) | copy-start | bytes 3244036
  48.3 23.0 %copy-start.3 = (bf16[32,2048]{1,0:T(8,128)(2,1)S(1)}, bf16[32,2048]{1,0:T(8,128)(2,1)}, u32[]{:S(2)}) copy-start(bf16[32,2048]{1,0:T(8,128)(2,1)} %hid_ref.3) | copy-start | bytes 393220

commit v2 on v1

--- a/solution.py
+++ b/solution.py
@@ -29,9 +29,9 @@
 
 
 def prefix_kernel(n_head, nope, rope, log2_scale, hid_ref, cos_ref, sin_ref, wq_hbm, wuk_hbm, kv_hbm,
-                  qs_ref, own_ref, x_ref, y_ref,
-                  hid_all, cos_all, sin_all, wq_v, wuk_v, kv_v, q_v, qs_f, m_v, l_v, s_v, p_v, diag, carry,
-                  wq_sem, own_sem, send_sem, recv_sem):
+                  qs_hbm, own_hbm, x_hbm, y_hbm, soon_x_hbm, soon_y_hbm,
+                  hid_all, cos_all, sin_all, wq_v, wuk_v, kv_v, q_v, qs_f, qs_v, m_v, l_v, s_v, p_v,
+                  own_v, x_v, y_v, diag, carry, wq_sem, own_sem, out_sem, send_sem, recv_sem):
     rows = hid_ref.shape[0]
     lat = wuk_v.shape[2]
     qk = nope + rope
@@ -41,6 +41,8 @@
     half = n_head // 2
     block = half * rows
     chunk = s_v.shape[2]
+    soon = soon_x_hbm.shape[0]
+    rest = block + TAIL - soon
     me = lax.axis_index('ctx')
     core = lax.rem(me, 2)
     xx = lax.rem(me // 2, 2)
@@ -105,19 +107,25 @@
         for p in range(3):
             keep(p, h, q_lat[p * rows:(p + 1) * rows], q_rot[p * rows:(p + 1) * rows])
 
-    def attend(peer, o_ref):
-        for n in range(2):
+    def attend(targets, between=()):
+        for b, o_ref, n in targets:
             o_ref[n, 0:block] = jnp.zeros((block, lat), F32)
-            m_v[2 * peer + n] = jnp.full((block, 128), -jnp.inf, F32)
-            l_v[2 * peer + n] = jnp.zeros((block, 128), F32)
+            m_v[b] = jnp.full((block, 128), -jnp.inf, F32)
+            l_v[b] = jnp.zeros((block, 128), F32)
+        for copy in between:
+            copy.start()
 
         def visit(i, _):
             keys = pl.ds(pl.multiple_of(i * chunk, chunk), chunk)
-            items = [(k, n) for k in range(2) for n in range(2)]
-            for t, (k, n) in enumerate(items):
-                s_v[t] = jnp.dot(q_v[2 * peer + n], kv_v[k, :, keys], preferred_element_type=F32)
-            for t, (k, n) in enumerate(items):
-                b = 2 * peer + n
+            items = [(k, *target) for k in range(2) for target in targets]
+            def score(t):
+                k, b = items[t][:2]
+                s_v[t] = jnp.dot(q_v[b], kv_v[k, :, keys], preferred_element_type=F32)
+
+            score(0)
+            for t, (k, b, o_ref, n) in enumerate(items):
+                if t + 1 < len(items):
+                    score(t + 1)
                 for r in range(0, block, 64):
                     at = slice(r, r + 64)
                     s = s_v[t, at]
@@ -137,15 +145,13 @@
 
         lax.fori_loop(0, kv_v.shape[2] // chunk, visit, 0)
 
-    def close(peer, o_ref):
-        for n in range(2):
-            b = 2 * peer + n
+    def close(targets):
+        for b, o_ref, n in targets:
             o_ref[n, block:block + TAIL, 0:block] = jnp.transpose(m_v[b])[0:TAIL]
             l_sum = jnp.broadcast_to(jnp.sum(l_v[b], axis=1, keepdims=True), (block, 128))
             o_ref[n, block:block + TAIL, block:2 * block] = jnp.transpose(l_sum)[0:TAIL]
 
-    def merge(peer, n, o_ref, c):
-        b = 2 * peer + n
+    def merge(b, o_ref, n, c):
         m_in = jnp.broadcast_to(jnp.transpose(carry[c, block:block + TAIL, 0:block])[:, 0:1], (block, 128))
         l_in = jnp.transpose(carry[c, block:block + TAIL, block:2 * block])[:, 0:1]
         m_new = jnp.maximum(m_v[b], m_in)
@@ -162,12 +168,16 @@
             wuk_copy.wait()
         project(hid_ref[...], cos_ref[...], sin_ref[...], g, store_own)
     for n in range(lat // 128):
-        qs_ref[:, n * 128:(n + 1) * 128] = qs_f[n].astype(BF16)
-    qs_ref[:, lat:lat + rope] = qs_f[lat // 128][:, 0:rope].astype(BF16)
+        qs_v[:, n * 128:(n + 1) * 128] = qs_f[n].astype(BF16)
+    qs_v[:, lat:lat + rope] = qs_f[lat // 128][:, 0:rope].astype(BF16)
     kv_copy.wait()
     kv_send.wait()
-    attend(3, own_ref)
-    close(3, own_ref)
+    outs = [pltpu.make_async_copy(qs_v, qs_hbm, out_sem.at[0])]
+    own_targets, d_targets = [(6, own_v, 0), (7, own_v, 1)], [(4, diag, 0), (5, diag, 1)]
+    plain, added = [(0, x_v, 0), (3, y_v, 1)], [(1, x_v, 1), (2, y_v, 0)]
+    attend(own_targets, between=outs)
+    close(own_targets)
+    outs.append(pltpu.make_async_copy(own_v, own_hbm, out_sem.at[5]))
 
     for copy in gathers:
         copy.wait()
@@ -177,22 +187,29 @@
     for g in range(groups):
         project(hid3, cos3, sin3, g, store_peer)
 
-    attend(2, diag)
-    close(2, diag)
+    attend(d_targets)
+    close(d_targets)
     over = [remote(diag.at[0], carry.at[0], 10, to_x), remote(diag.at[1], carry.at[1], 11, to_y)]
-    for copy in over:
-        copy.start()
-    attend(0, x_ref)
-    attend(1, y_ref)
+    attend(plain, between=[*over, outs[1]])
+    close(plain)
+    early = [remote(x_v.at[0, 0:soon], soon_x_hbm, 12, to_x), remote(y_v.at[1, 0:soon], soon_y_hbm, 13, to_y)]
+    outs.append(pltpu.make_async_copy(x_v.at[0, soon:block + TAIL], x_hbm.at[0:rest], out_sem.at[1]))
+    outs.append(pltpu.make_async_copy(y_v.at[1, soon:block + TAIL], y_hbm.at[block + TAIL:rest + block + TAIL], out_sem.at[2]))
+    attend(added, between=[*early, *outs[2:]])
     for copy in over:
         copy.wait()
-    merge(1, 0, y_ref, 0)
-    merge(0, 1, x_ref, 1)
-    close(0, x_ref)
-    close(1, y_ref)
-
-
-def prefix_phase(hidden, w_q, w_uk, kv_own, seq_lens, first_pos, log2_scale, chunk=1024):
+    merge(1, x_v, 1, 1)
+    merge(2, y_v, 0, 0)
+    close(added)
+    last = [pltpu.make_async_copy(x_v.at[1], x_hbm.at[rest:rest + block + TAIL], out_sem.at[3]),
+            pltpu.make_async_copy(y_v.at[0], y_hbm.at[0:block + TAIL], out_sem.at[4])]
+    for copy in last:
+        copy.start()
+    for copy in (*outs, *early, *last):
+        copy.wait()
+
+
+def prefix_phase(hidden, w_q, w_uk, kv_own, seq_lens, first_pos, log2_scale, chunk=1024, soon=32):
     rows, dim = hidden.shape
     n_head, nope, lat = w_uk.shape
     qk = w_q.shape[1] // n_head
@@ -201,45 +218,53 @@
     angle = (first_pos + seq_lens).astype(F32)[:, None] * inv_freq
     block = n_head // 2 * rows
     payload = jax.ShapeDtypeStruct((2, block + TAIL, lat), F32)
+    early = jax.ShapeDtypeStruct((soon, lat), F32)
+    later = jax.ShapeDtypeStruct((2 * (block + TAIL) - soon, lat), F32)
     in_hbm = pl.BlockSpec(memory_space=pltpu.HBM)
     return pl.pallas_call(
         functools.partial(prefix_kernel, n_head, nope, rope, log2_scale),
-        out_shape=(jax.ShapeDtypeStruct((rows * n_head, lat + rope), BF16), payload, payload, payload),
+        out_shape=(jax.ShapeDtypeStruct((rows * n_head, lat + rope), BF16), payload, later, later, early, early),
         in_specs=[vmem(), vmem(), vmem(), in_hbm, in_hbm, in_hbm],
-        out_specs=(vmem(), vmem(), vmem(), vmem()),
+        out_specs=(in_hbm,) * 6,
         scratch_shapes=[
             pltpu.VMEM((3, rows, dim), BF16), pltpu.VMEM((3, rows, rope // 2), F32), pltpu.VMEM((3, rows, rope // 2), F32),
             pltpu.VMEM(w_q.shape, BF16), pltpu.VMEM(w_uk.shape, BF16), pltpu.VMEM((2, *kv_own.shape), BF16),
             pltpu.VMEM((8, block, lat + rope), BF16), pltpu.VMEM((lat // 128 + 1, rows * n_head, 128), F32),
+            pltpu.VMEM((rows * n_head, lat + rope), BF16),
             pltpu.VMEM((8, block, 128), F32), pltpu.VMEM((8, block, 128), F32),
             pltpu.VMEM((4, block, chunk), F32), pltpu.VMEM((4, block, chunk), BF16),
-            pltpu.VMEM(payload.shape, F32), pltpu.VMEM(payload.shape, F32),
-            pltpu.SemaphoreType.DMA((n_head // 4,)), pltpu.SemaphoreType.DMA((2,)),
-            pltpu.SemaphoreType.DMA((12,)), pltpu.SemaphoreType.DMA((12,))],
+            *[pltpu.VMEM(payload.shape, F32)] * 5,
+            pltpu.SemaphoreType.DMA((n_head // 4,)), pltpu.SemaphoreType.DMA((2,)), pltpu.SemaphoreType.DMA((6,)),
+            pltpu.SemaphoreType.DMA((14,)), pltpu.SemaphoreType.DMA((14,))],
         compiler_params=pltpu.CompilerParams(collective_id=0, has_side_effects=True, vmem_limit_bytes=60 * MIB),
         name='prefix',
     )(hidden, jnp.cos(angle), jnp.sin(angle), w_q, w_uk, kv_own)
 
 
-def suffix_kernel(log2_scale, lat, chunk, unit, ring, lens_ref, q_ref, kv_hbm, o_ref, m_ref, l_ref,
-                  kv_v, s_v, m_v, l_v, acc, sems, b_s, c_s):
+def suffix_kernel(log2_scale, lat, chunk, unit, ring, streamed, lens_ref, q_hbm, kv_hbm, o_ref, m_ref, l_ref,
+                  q_ref, kv_v, s_v, m_v, l_v, acc, sems, q_sem, b_s, c_s):
     n_seq = lens_ref.shape[0]
-    heads = q_ref.shape[0] // n_seq
+    heads = q_hbm.shape[0] // n_seq
     shift = chunk.bit_length() - 1
+    q_copy = pltpu.make_async_copy(q_hbm, q_ref, q_sem)
+    q_copy.start()
     total = jnp.int32(0)
     for b in range(n_seq):
         total += lax.shift_right_logical(lens_ref[b], shift) + 1
     trips = lax.div(total + unit - 1, unit)
     depth = ring - 2
 
-    def start(at, group):
+    def start(at, group, live):
         b, c = at
         for u in range(unit):
             b_s[group * unit + u] = b
             c_s[group * unit + u] = c
             have = jnp.minimum(b, n_seq - 1)
-            pltpu.make_async_copy(
-                kv_hbm.at[have, :, pl.ds(pl.multiple_of(c * chunk, chunk), chunk)], kv_v.at[group, u], sems.at[group]).start()
+
+            @pl.when(live)
+            def _(u=u, c=c, have=have):
+                pltpu.make_async_copy(
+                    kv_hbm.at[have, :, pl.ds(pl.multiple_of(c * chunk, chunk), chunk)], kv_v.at[group, u], sems.at[group]).start()
             last = c >= lax.shift_right_logical(lens_ref[have], shift)
             b, c = jnp.where(last, jnp.minimum(b + 1, n_seq), b), jnp.where(last, 0, c + 1)
         return b, c
@@ -247,11 +272,10 @@
     for u in range(unit):
         b_s[(ring - 1) * unit + u] = n_seq
         c_s[(ring - 1) * unit + u] = 0
-    ahead = lax.fori_loop(0, jnp.minimum(depth, trips), lambda j, at: start(at, j), (jnp.int32(0), jnp.int32(0)))
+    ahead = lax.fori_loop(0, depth, lambda j, at: start(at, j, j < trips), (jnp.int32(0), jnp.int32(0)))
 
     def step(i, at):
         base, prev, far = [lax.rem(i + d, ring) for d in (0, ring - 1, depth)]
-        at = lax.cond(i + depth < trips, lambda: start(at, far), lambda: at)
 
         @pl.when(i < trips)
         def _():
@@ -280,7 +304,10 @@
             part = p[:, 0:128]
             for n in range(1, chunk // 128):
                 part += p[:, n * 128:(n + 1) * 128]
-            added = lax.dot_general(p.astype(BF16), kv_v[prev, u, 0:lat, :], NT, preferred_element_type=F32)
+            if u in streamed:
+                added = jnp.transpose(lax.dot_general(kv_v[prev, u, 0:lat, :], p.astype(BF16), NT, preferred_element_type=F32))
+            else:
+                added = lax.dot_general(p.astype(BF16), kv_v[prev, u, 0:lat, :], NT, preferred_element_type=F32)
             l_old = jnp.where(first, 0.0, l_old * alpha) + part
             o_old = jnp.where(first, 0.0, o_old * wide(alpha, lat // 128)) + added
             m_old = m_new
@@ -290,25 +317,26 @@
             for n in range(lat // 128):
                 o_ref[n, out, :] = o_old[:, n * 128:(n + 1) * 128]
         m_v[...], l_v[...], acc[...] = m_old, l_old, o_old
-        return at
-
+        return start(at, far, i + depth < trips)
+
+    q_copy.wait()
     lax.fori_loop(0, trips + 1, step, ahead)
 
 
-def suffix_part(q_seq, kv_suffix, seq_lens, log2_scale, lat, chunk=256, unit=8, ring=5):
+def suffix_part(q_seq, kv_suffix, seq_lens, log2_scale, lat, chunk=256, unit=8, ring=5, streamed=(1, 3, 5)):
     n_seq, slots, wide_row = kv_suffix.shape
     rows = q_seq.shape[0]
     heads = rows // n_seq
     flops = 2 * rows * slots * (wide_row + lat) * 4
     return pl.pallas_call(
-        functools.partial(suffix_kernel, log2_scale, lat, chunk, unit, ring),
+        functools.partial(suffix_kernel, log2_scale, lat, chunk, unit, ring, streamed),
         out_shape=(jax.ShapeDtypeStruct((lat // 128, rows + heads, 128), F32), jax.ShapeDtypeStruct((rows + heads, 128), F32),
                    jax.ShapeDtypeStruct((rows + heads, 128), F32)),
-        in_specs=[pl.BlockSpec(memory_space=pltpu.SMEM), vmem(), hbm()],
+        in_specs=[pl.BlockSpec(memory_space=pltpu.SMEM), hbm(), hbm()],
         out_specs=(vmem(), vmem(), vmem()),
-        scratch_shapes=[pltpu.VMEM((ring, unit, wide_row, chunk), BF16), pltpu.VMEM((2, unit, heads, chunk), F32),
+        scratch_shapes=[pltpu.VMEM(q_seq.shape, BF16), pltpu.VMEM((ring, unit, wide_row, chunk), BF16), pltpu.VMEM((2, unit, heads, chunk), F32),
                         pltpu.VMEM((heads, 128), F32), pltpu.VMEM((heads, 128), F32),
-                        pltpu.VMEM((heads, lat), F32), pltpu.SemaphoreType.DMA((ring,)),
+                        pltpu.VMEM((heads, lat), F32), pltpu.SemaphoreType.DMA((ring,)), pltpu.SemaphoreType.DMA,
                         pltpu.SMEM((ring * unit,), jnp.int32), pltpu.SMEM((ring * unit,), jnp.int32)],
         compiler_params=pltpu.CompilerParams(vmem_limit_bytes=32 * MIB),
         cost_estimate=pl.CostEstimate(flops=flops, bytes_accessed=40 * MIB, transcendentals=0),
@@ -316,27 +344,38 @@
     )(seq_lens, q_seq, kv_suffix.swapaxes(1, 2))
 
 
-def output_kernel(log2_scale, hid_ref, wuv_ref, wo_ref, so_ref, sm_ref, sl_ref, own_ref, x_ref, y_ref, out_ref, v_v):
+def output_kernel(log2_scale, hid_ref, wuv_ref, wo_ref, so_ref, sm_ref, sl_ref, own_ref, x_ref, y_ref, soon_x_ref, soon_y_ref, out_ref):
     n_head = wuv_ref.shape[0]
     rows = hid_ref.shape[0]
     half = n_head // 2
     block = half * rows
     value = wuv_ref.shape[2]
-    parts = [[(own_ref, n), (x_ref, n), (y_ref, n)] for n in range(2)]
+    soon = soon_x_ref.shape[0]
+    rest = block + TAIL - soon
+
+    def sums_of(side, at):
+        early = at < soon
+        from_x = x_ref[rest + at:rest + at + rows] if side else soon_x_ref[at:at + rows] if early else x_ref[at - soon:at - soon + rows]
+        low = block + TAIL + at - soon
+        from_y = y_ref[at:at + rows] if not side else soon_y_ref[at:at + rows] if early else y_ref[low:low + rows]
+        return own_ref[side, at:at + rows], from_x, from_y
+
     cols = []
-    for side in parts:
-        for ref, n in side:
-            m_t = jnp.transpose(ref[n, block:block + TAIL, 0:block])
-            l_t = jnp.transpose(ref[n, block:block + TAIL, block:2 * block])
-            cols.append((m_t[:, 0:1], l_t[:, 0:1]))
+    for side in range(2):
+        x_low = rest + block if side else block - soon
+        y_low = block + TAIL + block - soon if side else block
+        for tail in (own_ref[side, block:block + TAIL], x_ref[x_low:x_low + TAIL], y_ref[y_low:y_low + TAIL]):
+            cols.append((jnp.transpose(tail[:, 0:block])[:, 0:1], jnp.transpose(tail[:, block:2 * block])[:, 0:1]))
+    out = hid_ref[...].astype(F32)
+    values = []
     for h in range(n_head):
         side, at = h // half, (h % half) * rows
         mine = pl.ds(h, rows, stride=n_head)
         own = jnp.concatenate([so_ref[n, mine, :] for n in range(so_ref.shape[0])], axis=1)
         terms = [(own, sm_ref[mine, :][:, 0:1], jnp.sum(sl_ref[mine, :], axis=1, keepdims=True))]
-        for k, (ref, n) in enumerate(parts[side]):
+        for k, o_part in enumerate(sums_of(side, at)):
             m_part, l_part = cols[side * 3 + k]
-            terms.append((ref[n, at:at + rows, :], m_part[at:at + rows], l_part[at:at + rows]))
+            terms.append((o_part, m_part[at:at + rows], l_part[at:at + rows]))
         m_all = functools.reduce(jnp.maximum, [t[1] for t in terms])
         o_sum, l_sum = 0.0, 0.0
         for o_part, m_part, l_part in terms:
@@ -344,8 +383,11 @@
             o_sum += o_part * weight
             l_sum += l_part * weight
         o_lat = (o_sum / l_sum).astype(BF16)
-        v_v[:, h * value:(h + 1) * value] = jnp.dot(o_lat, wuv_ref[h], preferred_element_type=F32).astype(BF16)
-    out = hid_ref[...].astype(F32) + jnp.dot(v_v[...], wo_ref[...], preferred_element_type=F32)
+        values.append(jnp.dot(o_lat, wuv_ref[h], preferred_element_type=F32).astype(BF16))
+        if len(values) == 4:
+            low = (h - 3) * value
+            out += jnp.dot(jnp.concatenate(values, axis=1), wo_ref[low:low + 4 * value], preferred_element_type=F32)
+            values = []
     out_ref[...] = out.astype(BF16)
 
 
@@ -353,9 +395,8 @@
     return pl.pallas_call(
         functools.partial(output_kernel, log2_scale),
         out_shape=jax.ShapeDtypeStruct(hidden.shape, BF16),
-        in_specs=[vmem()] * 9,
+        in_specs=[vmem()] * 11,
         out_specs=vmem(),
-        scratch_shapes=[pltpu.VMEM((hidden.shape[0], w_o.shape[0]), BF16)],
         compiler_params=pltpu.CompilerParams(vmem_limit_bytes=32 * MIB),
         name='output',
     )(hidden, w_uv, w_o, *suffix, *parts)
@@ -373,9 +414,9 @@
         n_head = w_uk.shape[0]
         log2_scale = LOG2E * (w_q.shape[1] // n_head) ** -0.5
         kv_own = kv_prefix.swapaxes(0, 1)
-        q_seq, own, to_x, to_y = prefix_phase(hidden, w_q, w_uk, kv_own, seq_lens, kv_prefix.shape[0] * group, log2_scale)
+        q_seq, own, to_x, to_y, soon_x, soon_y = prefix_phase(hidden, w_q, w_uk, kv_own, seq_lens, kv_prefix.shape[0] * group, log2_scale)
         got_x, got_y = lax.ppermute(to_x, 'ctx', over_x), lax.ppermute(to_y, 'ctx', over_y)
         suffix = suffix_part(q_seq, kv_suffix, seq_lens, log2_scale, lat)
-        return finish_output(hidden, w_uv, w_o, suffix, (own, got_x, got_y), log2_scale)
+        return finish_output(hidden, w_uv, w_o, suffix, (own, got_x, got_y, soon_x, soon_y), log2_scale)
 
     return jax.shard_map(local_step, mesh=mesh, in_specs=(rows_spec, whole_spec, whole_spec, whole_spec, whole_spec, rows_spec, P(('dp', 'ctx'), None, None), P(('dp', 'ctx'))), out_specs=rows_spec, check_vma=False)

time: 75.2 us -> 73.7 us (0.980)
  waiting for transfers between devices: 4.04 us -> 0.01 us
  Pallas kernels: 66.3 us -> 69.2 us
    pallas_call x1, Pallas kernels: 18.9 us -> 21.9 us  [suffix_part(): pl.pallas_call(functools.partial(suffix_kernel, log2_scale, lat, chunk, u...]
    ppermute x1, waiting for transfers between devices: 2.83 us -> 0.01 us  [local_step(): lax.ppermute(to_x, 'ctx', over_x)]
    ppermute x1, waiting for transfers between devices: 1.21 us -> 0.01 us  [local_step(): lax.ppermute(to_y, 'ctx', over_y)]
  transfers between devices with their start and end apart: 2 -> 2, of which waited for: 2 -> 0; matrix products, arithmetic and copies ran while one was open for 0% -> 0% of each run, Pallas kernels for 25% -> 30%
where the time goes in v2:
time: 73.7 us; the launch traced here: 74.1 us
  Pallas kernels  69.2 us (94%)
  starting transfers between devices  2.05 us (3%)
  other arithmetic  1.42 us (2%)
  local copies, waits for them, and re-layouts  1.27 us (2%)
    pallas_call x1, Pallas kernels, prefix_phase(): pl.pallas_call(functools.partial(prefix_kernel, n_head, nope, rope, log2_...  43.8 us
    pallas_call x1, Pallas kernels, suffix_part(): pl.pallas_call(functools.partial(suffix_kernel, log2_scale, lat, chunk, u...  21.9 us
    pallas_call x1, Pallas kernels, finish_output(): pl.pallas_call(functools.partial(output_kernel, log2_scale), out_shape=ja...  3.5 us
    ppermute x1, starting transfers between devices, local_step(): lax.ppermute(to_x, 'ctx', over_x)  1.51 us
  transfers between devices with their start and end apart: 2, of which 0 were waited for; matrix products, arithmetic and copies ran while one was open for 0% of the time, Pallas kernels for 30%

profile of v2, /device:TPU:0, one launch (start us, length us, event | category | flops | bytes accessed | tf_op | source)
XLA Modules:
  0.0 74.1 jit_solution(15868681814710913010)
XLA Ops:
  0.0 0.7 add_convert_fusion
  0.7 0.8 %multiply_sine_fusion = (f32[32,32]{1,0:T(8,128)}, f32[32,32]{1,0:T(8,128)}) fusion(f32[32]{0:T(128)S(1)} %multiply_exponential_fusion, f32[32]{0:T(128)S(1)} %add_convert_fusion), kind=kLoop, calls=%fused_computation | loop fusion | flops 1024 | bytes 8448 | tf_op jit(solution)/shard_map/sin | solution.py:241
  1.4 0.0 copy-start.6
  1.4 43.8 %prefix.1 = (bf16[512,576]{1,0:T(8,128)(2,1)}, f32[2,264,512]{2,1,0:T(8,128)}, f32[496,512]{1,0:T(8,128)}, f32[496,512]{1,0:T(8,128)}, f32[32,512]{1,0:T(8,128)}, /*index=5*/f32[32,512]{1,0:T(8,128)}) custom-call(bf16[32,2048]{1,0:T(8,128)(2,1)} %hid_ref.3, f32[32,32]{1,0:T(8,128)} %get-tuple-element.24.cos_ref, f32[32,32]{1,0:T(8,128)} %get-tuple-element.23.sin_ref, ...), custom_call_target="tpu_custom_call" | custom-call | tf_op jit(solution)/shard_map/prefix/pallas_call | solution.py:224
  45.3 1.5 %collective-permute-start = (f32[496,512]{1,0:T(8,128)}, f32[496,512]{1,0:T(8,128)S(1)}, u32[]{:S(2)}, u32[]{:S(2)}) collective-permute-start(f32[496,512]{1,0:T(8,128)} %get-tuple-element.19), channel_id=1, source_target_pairs={{0,2},{1,3},{2,0},{3,1},{4,6},{5,7},{6,4},{7,5}} | collective-permute-start | bytes 3047432 | tf_op jit(solution)/shard_map/ppermute | solution.py:418
  46.8 0.5 collective-permute-start.1
  47.3 0.0 slice-start
  47.3 0.0 copy-done.6
  47.3 0.0 copy-start.2
  47.3 1.2 %copy-done.2 = bf16[512,576]{1,0:T(8,128)(2,1)S(1)} copy-done((bf16[512,576]{1,0:T(8,128)(2,1)S(1)}, bf16[512,576]{1,0:T(8,128)(2,1)}, u32[]{:S(2)}) %copy-start.2) | copy-done | bytes 589848
  48.6 0.0 slice-start.1
  48.6 0.0 copy-start
  48.6 0.0 copy-start.1
  48.6 0.0 copy-start.3
  48.6 0.0 copy-start.4
  48.6 0.0 copy-start.5
  48.6 21.9 %suffix.1 = (f32[4,528,128]{2,1,0:T(8,128)S(1)}, f32[528,128]{1,0:T(8,128)S(1)}, f32[528,128]{1,0:T(8,128)S(1)}) custom-call(s32[32]{0:T(128)S(1)} %copy-done.6, bf16[512,576]{1,0:T(8,128)(2,1)S(1)} %copy-done.2, bf16[32,576,2048]{2,1,0:T(8,128)(2,1)} %bitcast.1.kv_hbm), custom_call_target="tpu_custom_call" | custom-call | flops 9126805504 | bytes 41943040 | tf_op jit(solution)/shard_map/suffix/pallas_call | solution.py:331
  70.5 0.0 collective-permute-done.x_ref
  70.5 0.0 collective-permute-done.1.y_ref
  70.5 0.0 slice-done
  70.5 0.0 slice-done.1
  70.5 0.0 copy-done
  70.5 0.0 copy-done.1
  70.5 0.0 copy-done.3
  70.5 0.0 copy-done.4
  70.6 0.0 copy-done.5
  70.6 3.5 %output.1 = bf16[32,2048]{1,0:T(8,128)(2,1)} custom-call(bf16[32,2048]{1,0:T(8,128)(2,1)S(1)} %copy-done.3, bf16[16,512,128]{2,1,0:T(8,128)(2,1)S(1)} %copy-done, bf16[2048,2048]{1,0:T(8,128)(2,1)S(1)} %bitcast.3, f32[4,528,128]{2,1,0:T(8,128)S(1)} %get-tuple-element.15.so_ref, f32[528,128]{1,0:T(8,128)S(1)} %get-tuple-element.16.sm_ref, ...), custom_call_target="tpu_custom_call" | custom-call | tf_op jit(solution)/shard_map/output/pallas_call | solution.py:395
  (2 shorter events, 0.0 us)
Async XLA Ops:
  1.4 45.9 %copy-start.6 = (s32[32]{0:T(128)S(1)}, s32[32]{0:T(128)}, u32[]{:S(2)}) copy-start(s32[32]{0:T(128)} %lens_ref.1) | copy-start | bytes 388
  45.3 25.2 %collective-permute-start = (f32[496,512]{1,0:T(8,128)}, f32[496,512]{1,0:T(8,128)S(1)}, u32[]{:S(2)}, u32[]{:S(2)}) collective-permute-start(f32[496,512]{1,0:T(8,128)} %get-tuple-element.19), channel_id=1, source_target_pairs={{0,2},{1,3},{2,0},{3,1},{4,6},{5,7},{6,4},{7,5}} | collective-permute-start | bytes 3047432 | tf_op jit(solution)/shard_map/ppermute | solution.py:418
  46.8 23.7 %collective-permute-start.1 = (f32[496,512]{1,0:T(8,128)}, f32[496,512]{1,0:T(8,128)S(1)}, u32[]{:S(2)}, u32[]{:S(2)}) collective-permute-start(f32[496,512]{1,0:T(8,128)} %get-tuple-element.20), channel_id=1, source_target_pairs={{0,4},{1,5},{2,6},{3,7},{4,0},{5,1},{6,2},{7,3}} | collective-permute-start | bytes 3047432 | tf_op jit(solution)/shard_map/ppermute | solution.py:418
  47.3 23.2 %slice-start = ((s8[8388608]{0:T(1024)(128)(4,1)}), s8[4194304]{0:T(1024)(128)(4,1)S(1)}, s32[]{:S(2)}) async-start(s8[8388608]{0:T(1024)(128)(4,1)} %bitcast.2), calls=%async_computation | async-start | bytes 8388608
  47.3 1.2 %copy-start.2 = (bf16[512,576]{1,0:T(8,128)(2,1)S(1)}, bf16[512,576]{1,0:T(8,128)(2,1)}, u32[]{:S(2)}) copy-start(bf16[512,576]{1,0:T(8,128)(2,1)} %get-tuple-element.14.q_hbm) | copy-start | bytes 1769476
  48.6 21.9 %slice-start.1 = ((s8[8388608]{0:T(1024)(128)(4,1)}), s8[4194304]{0:T(1024)(128)(4,1)S(1)}, s32[]{:S(2)}) async-start(s8[8388608]{0:T(1024)(128)(4,1)} %bitcast.2), calls=%async_computation.1 | async-start | bytes 8388608
  48.6 22.0 %copy-start = (bf16[16,512,128]{2,1,0:T(8,128)(2,1)S(1)}, bf16[16,512,128]{2,1,0:T(8,128)(2,1)}, u32[]{:S(2)}) copy-start(bf16[16,512,128]{2,1,0:T(8,128)(2,1)} %wuv_ref.1) | copy-start | bytes 6291460
  48.6 22.0 %copy-start.1 = (f32[2,264,512]{2,1,0:T(8,128)S(1)}, f32[2,264,512]{2,1,0:T(8,128)}, u32[]{:S(2)}) copy-start(f32[2,264,512]{2,1,0:T(8,128)} %get-tuple-element.18.own_ref) | copy-start | bytes 3244036
  48.6 22.0 %copy-start.3 = (bf16[32,2048]{1,0:T(8,128)(2,1)S(1)}, bf16[32,2048]{1,0:T(8,128)(2,1)}, u32[]{:S(2)}) copy-start(bf16[32,2048]{1,0:T(8,128)(2,1)} %hid_ref.3) | copy-start | bytes 393220
  48.6 22.0 %copy-start.4 = (f32[32,512]{1,0:T(8,128)S(1)}, f32[32,512]{1,0:T(8,128)}, u32[]{:S(2)}) copy-start(f32[32,512]{1,0:T(8,128)} %get-tuple-element.21.soon_x_ref) | copy-start | bytes 196612
  48.6 22.0 %copy-start.5 = (f32[32,512]{1,0:T(8,128)S(1)}, f32[32,512]{1,0:T(8,128)}, u32[]{:S(2)}) copy-start(f32[32,512]{1,0:T(8,128)} %get-tuple-element.22.soon_y_ref) | copy-start | bytes 196612
